TPU v7x, 32 devices: a whole 2x2x4 slice. The times are simulated.
32 devices in a mesh: blk: 8 (over z, x), col: 4 (over y, core).
Axes of the slice: x: 2, y: 2, z: 4, core: 2. Of those that a mesh axis runs over, the one named last changes fastest.
Arguments:
- pixel_row: int32 [2048, 256], P(('blk', 'col')), may hold values from 0 to 63, as said below
- pixel_col: int32 [2048, 256], P(('blk', 'col')), may hold values from 0 to 2047, as said below
- strip_of_span: int32 [32, 64], P(('blk', 'col')), may hold values from 0 to 31, as said below
- shear_one: float32 [2048, 256], P(('blk', 'col')), may hold values from -6 to 6
- shear_two: float32 [2048, 256], P(('blk', 'col')), may hold values from -6 to 6
- weight: float32 [2048, 256], P(('blk', 'col')), may hold values from 0.25 to 4
Outputs:
- kappa_e: float32 [2048, 8192], P(('blk', 'col'))
- kappa_b: float32 [2048, 8192], P(('blk', 'col'))
Inputs may be any that keep to these rules, and one draw needn't show every extreme that they name: `pixel_row`: all galaxies of one span (one row) lie in one aligned band of 8 rows. `pixel_col`: all galaxies of one span (one row) lie in one aligned block of 128 columns. `strip_of_span`: row d names the row strip of each span of shard d; each strip is named exactly 2 times in every row.
All inputs are finite; a program needn't handle non-finite values.
Results may differ from a plain program's by a relative error of at most 0.0038.
Values may be sent and summed in bfloat16 or wider, within the bound.
A program may use at most 128 MiB of HBM per device.

v0:
```python
import math

import jax
import jax.numpy as jnp
import numpy as np
from jax import lax
from jax.experimental import pallas as pl
from jax.experimental.pallas import tpu as pltpu
from jax.sharding import PartitionSpec as P

SLAB = 256
TILE_COLS = 2048
BAND = 8
SUBC = 128
DEPTH = 2


highest = lax.Precision.HIGHEST


def factor_pair(length):
    return (length // 128, 128)


def complex_table(left_len, right_len, modulus, direction):
    first_idx = lax.broadcasted_iota(jnp.int32, (left_len, right_len), 0)
    second_idx = lax.broadcasted_iota(jnp.int32, (left_len, right_len), 1)
    angles = (
        direction * 2.0 * math.pi / modulus * (first_idx * second_idx % modulus).astype(jnp.float32)
    )
    cosine = jnp.cos(angles)
    sine_part = jnp.sin(angles)
    return jnp.stack([jnp.stack([cosine, sine_part], -1), jnp.stack([-sine_part, cosine], -1)], 0)


def twiddle_parts(outer_len, inner_len, modulus, direction, factor):
    first_idx = lax.broadcasted_iota(jnp.int32, (outer_len, inner_len), 0)
    second_idx = lax.broadcasted_iota(jnp.int32, (outer_len, inner_len), 1)
    angles = (
        direction * 2.0 * math.pi / modulus * (first_idx * second_idx % modulus).astype(jnp.float32)
    )
    return (factor * jnp.cos(angles), factor * jnp.sin(angles))


def rotate(complex_field, cosine, sine_part):
    return jnp.stack(
        [
            complex_field[0] * cosine - complex_field[1] * sine_part,
            complex_field[0] * sine_part + complex_field[1] * cosine,
        ]
    )


def transform_rows(complex_field, direction):
    row_count = complex_field.shape[1]
    length = complex_field.shape[2]
    outer_len, inner_len = factor_pair(length)
    factor = 1.0 if direction < 0 else 1.0 / length
    cosine, sine_part = twiddle_parts(outer_len, inner_len, length, direction, factor)
    small_table = complex_table(outer_len, outer_len, outer_len, direction)
    large_table = complex_table(inner_len, inner_len, inner_len, direction)
    blocked = complex_field.reshape(2, row_count, outer_len, inner_len)
    if direction < 0:
        blocked = jnp.einsum("prab,pakq->qrkb", blocked, small_table, precision=highest)
        blocked = rotate(blocked, cosine, sine_part)
        blocked = jnp.einsum("prkb,pbsq->qrks", blocked, large_table, precision=highest)
    else:
        blocked = jnp.einsum("prks,psbq->qrkb", blocked, large_table, precision=highest)
        blocked = rotate(blocked, cosine, sine_part)
        blocked = jnp.einsum("prkb,pkaq->qrab", blocked, small_table, precision=highest)
    return blocked.reshape(2, row_count, length)


def transform_columns(complex_field, direction):
    length = complex_field.shape[1]
    col_count = complex_field.shape[2]
    outer_len, inner_len = factor_pair(length)
    factor = 1.0 if direction < 0 else 1.0 / length
    cosine, sine_part = twiddle_parts(outer_len, inner_len, length, direction, factor)
    cosine = cosine[:, :, None]
    sine_part = sine_part[:, :, None]
    small_table = complex_table(outer_len, outer_len, outer_len, direction)
    large_table = complex_table(inner_len, inner_len, inner_len, direction)
    blocked = complex_field.reshape(2, outer_len, inner_len, col_count)
    if direction < 0:
        blocked = jnp.einsum("pabw,pakq->qkbw", blocked, small_table, precision=highest)
        blocked = rotate(blocked, cosine, sine_part)
        blocked = jnp.einsum("pkbw,pbsq->qksw", blocked, large_table, precision=highest)
    else:
        blocked = jnp.einsum("pksw,psbq->qkbw", blocked, large_table, precision=highest)
        blocked = rotate(blocked, cosine, sine_part)
        blocked = jnp.einsum("pkbw,pkaq->qabw", blocked, small_table, precision=highest)
    return blocked.reshape(2, length, col_count)


def signed_frequency(position, length):
    outer_len, inner_len = factor_pair(length)
    freq_index = position // inner_len + outer_len * (position % inner_len)
    signed = jnp.where(freq_index < length // 2, freq_index, freq_index - length)
    return signed.astype(jnp.float32) / length


def bin_region(rows_in, cols_in, values, region_rows, region_cols):
    span_count = rows_in.shape[0]
    galaxies = rows_in.shape[1]
    band_count = region_rows // BAND
    blocks = region_cols // SUBC
    position = rows_in[:, 0] // BAND * blocks + cols_in[:, 0] // SUBC
    group_size = math.gcd(span_count, 128)

    def one_group(unused, group_data):
        row_part, col_part, value_part = group_data
        row_hot = (row_part[:, None, :] == lax.broadcasted_iota(jnp.int32, (1, BAND, 1), 1)).astype(
            jnp.bfloat16
        )
        weighted = (value_part[:, :, None, :] * row_hot[:, None, :, :]).reshape(
            group_size, 3 * BAND, galaxies
        )
        col_hot = (col_part[:, :, None] == lax.broadcasted_iota(jnp.int32, (1, 1, SUBC), 2)).astype(
            jnp.bfloat16
        )
        return (
            unused,
            jnp.einsum("ckg,cgs->cks", weighted, col_hot, preferred_element_type=jnp.float32),
        )

    group_inputs = (
        (rows_in % BAND).reshape(-1, group_size, galaxies),
        (cols_in % SUBC).reshape(-1, group_size, galaxies),
        values.reshape(-1, group_size, 3, galaxies),
    )
    unused_carry, partials = lax.scan(one_group, jnp.zeros((), jnp.float32), group_inputs)
    partials = partials.reshape(span_count, 3 * BAND * SUBC)
    summed = jax.ops.segment_sum(partials, position, num_segments=band_count * blocks)
    summed = summed.reshape(band_count, blocks, 3, BAND, SUBC).transpose(2, 0, 3, 1, 4)
    summed = summed.reshape(3, region_rows, region_cols)
    floored = jnp.maximum(summed[0], 1.0)
    return jnp.stack([summed[1] / floored, summed[2] / floored])


def generic_local(pixel_row, pixel_col, strip_of_span, shear_one, shear_two, weight):
    tile_count = lax.axis_size("col")
    my_slab = lax.axis_index("blk")
    my_tile = lax.axis_index("col")
    strip_rows = SLAB // tile_count
    span_total = pixel_row.shape[0]
    by_strip = jnp.argsort(strip_of_span[0], stable=True)
    packed = jnp.take(pixel_row * TILE_COLS + pixel_col, by_strip, axis=0)
    values = jnp.stack(
        [
            weight.astype(jnp.bfloat16),
            (weight * shear_one).astype(jnp.bfloat16),
            (weight * shear_two).astype(jnp.bfloat16),
        ],
        axis=1,
    )
    values = jnp.take(values, by_strip, axis=0)
    arrival = jnp.arange(span_total, dtype=jnp.int32) // DEPTH
    own_cell, own_values = (
        lax.all_to_all(packed, ("blk", "col"), split_axis=0, concat_axis=0, tiled=True),
        lax.all_to_all(values, ("blk", "col"), split_axis=0, concat_axis=0, tiled=True),
    )
    rows_in = own_cell // TILE_COLS
    cols_in = (arrival % tile_count)[:, None] * TILE_COLS + own_cell % TILE_COLS
    whole_rows = bin_region(rows_in, cols_in, own_values, strip_rows, TILE_COLS * tile_count)
    row_spectrum = transform_rows(whole_rows, -1)
    total_cols = row_spectrum.shape[2]
    whole_cols = lax.all_to_all(
        row_spectrum, ("blk", "col"), split_axis=2, concat_axis=1, tiled=True
    )
    col_width = whole_cols.shape[2]
    first_col = (my_slab * tile_count + my_tile) * col_width
    spectrum = transform_columns(whole_cols, -1)
    total_rows = spectrum.shape[1]
    freq_y = signed_frequency(jnp.arange(total_rows, dtype=jnp.int32), total_rows)[:, None]
    freq_x = signed_frequency(first_col + jnp.arange(col_width, dtype=jnp.int32), total_cols)[
        None, :
    ]
    radius_sq = freq_x * freq_x + freq_y * freq_y
    safe_radius = jnp.where(radius_sq > 0, radius_sq, 1.0)
    kernel_re = (freq_x * freq_x - freq_y * freq_y) / safe_radius
    kernel_im = 2.0 * freq_x * freq_y / safe_radius
    kappa_hat = jnp.stack(
        [
            kernel_re * spectrum[0] + kernel_im * spectrum[1],
            kernel_re * spectrum[1] - kernel_im * spectrum[0],
        ]
    )
    col_result = transform_columns(kappa_hat, 1)
    back_rows = lax.all_to_all(col_result, ("blk", "col"), split_axis=1, concat_axis=2, tiled=True)
    convergence = transform_rows(back_rows, 1)
    return (convergence[0], convergence[1])


LANES = 128
CHANNELS = 6
VMEM_BYTES = 60 * 1024 * 1024


def split_hi_lo(x):
    hi = x.astype(jnp.bfloat16)
    return hi, (x - hi.astype(jnp.float32)).astype(jnp.bfloat16)


def fft_list(points, sign):
    n = len(points)
    if n == 1:
        return points
    even = fft_list(points[0::2], sign)
    odd = fft_list(points[1::2], sign)
    half = n // 2
    first, second = [], []
    root = math.sqrt(0.5)
    for k in range(half):
        er, ei = even[k]
        r, i = odd[k]
        if k == 0:
            tr, ti = r, i
            first.append((er + tr, ei + ti))
            second.append((er - tr, ei - ti))
            continue
        if 4 * k == n:
            if sign > 0:
                first.append((er - i, ei + r))
                second.append((er + i, ei - r))
            else:
                first.append((er + i, ei - r))
                second.append((er - i, ei + r))
            continue
        if 8 * k == n:
            tr, ti = (root * (r - sign * i), root * (i + sign * r)) if sign > 0 else (
                root * (r + i), root * (i - r))
        elif 8 * k == 3 * n:
            tr, ti = (-root * (r + i), root * (r - i)) if sign > 0 else (
                root * (i - r), -root * (r + i))
        else:
            c = math.cos(2 * math.pi * k / n)
            s = sign * math.sin(2 * math.pi * k / n)
            tr, ti = r * c - i * s, r * s + i * c
        first.append((er + tr, ei + ti))
        second.append((er - tr, ei - ti))
    return first + second


def np_real_form(length, direction, factor, transposed):
    idx = np.arange(length)
    ang = direction * 2 * np.pi / length * (np.outer(idx, idx) % length)
    c, s = factor * np.cos(ang), factor * np.sin(ang)
    full = np.block([[c, s], [-s, c]])
    full = (full.T if transposed else full).astype(np.float32)
    hi = full.astype(jnp.bfloat16)
    lo = (full - hi.astype(np.float32)).astype(jnp.bfloat16)
    return np.stack([hi, lo])


def np_twiddle(outer, inner, direction):
    ang = direction * 2 * np.pi / (outer * inner) * np.outer(np.arange(outer), np.arange(inner))
    return np.cos(ang).astype(np.float32), np.sin(ang).astype(np.float32)


def side_tables(outer):
    quarter = outer // 4
    pre = np.zeros((2, 2, quarter, 2), np.float32)
    tw = np.zeros((2, outer, LANES), np.float32)
    for side in range(2):
        for parity in range(2):
            residue = 2 * side + parity
            ang = -2 * np.pi * residue * np.arange(quarter) / outer
            pre[side, parity, :, 0], pre[side, parity, :, 1] = np.cos(ang), np.sin(ang)
            k = 4 * np.arange(quarter) + residue
            ang = -2 * np.pi / (outer * LANES) * np.outer(k, np.arange(LANES))
            at = parity * quarter
            tw[side, at : at + quarter] = np.cos(ang)
            tw[side, 2 * quarter + at : 2 * quarter + at + quarter] = np.sin(ang)
    return pre.reshape(-1), tw


def dot(a, b):
    return jnp.dot(a, b, preferred_element_type=jnp.float32)


def pack_kernel(row_ref, col_ref, strip_ref, one_ref, two_ref, weight_ref, out_ref, *, depth):
    spans = row_ref.shape[0]
    gal = row_ref.shape[1]
    strip_row = strip_ref[...]
    lane = lax.broadcasted_iota(jnp.int32, (spans, spans), 1)
    sub = lax.broadcasted_iota(jnp.int32, (spans, spans), 0)
    wide = jnp.broadcast_to(strip_row, (spans, spans))
    strip_col = jnp.sum(jnp.where(lane == sub, wide, 0), axis=1, keepdims=True)
    earlier = jnp.where((wide == strip_col) & (sub < lane), 1, 0)
    slot = strip_row * depth + jnp.sum(earlier, axis=0, keepdims=True)
    perm = jnp.where(slot == sub, 1.0, 0.0).astype(jnp.bfloat16)
    w = weight_ref[...]
    r = row_ref[...]
    c = col_ref[...]
    tile_blocks = TILE_COLS // SUBC
    pieces = (
        w.astype(jnp.bfloat16),
        (w * one_ref[...]).astype(jnp.bfloat16),
        (w * two_ref[...]).astype(jnp.bfloat16),
        (r % BAND).astype(jnp.float32).astype(jnp.bfloat16),
        (c % SUBC).astype(jnp.float32).astype(jnp.bfloat16),
        ((r // BAND) * tile_blocks + c // SUBC).astype(jnp.float32).astype(jnp.bfloat16),
    )
    for n, piece in enumerate(pieces):
        sorted_piece = dot(perm, piece).astype(jnp.bfloat16)
        out_ref[:spans, n * gal : (n + 1) * gal] = sorted_piece
        out_ref[spans:, n * gal : (n + 1) * gal] = sorted_piece


def rows_kernel(
    block_ref, band_ref, side_ref, pre_ref, spans_ref, tw_ref, table_ref, even_ref, odd_ref,
    spans32, acc, mid,
):
    spans = spans_ref.shape[0]
    gal = spans_ref.shape[1] // CHANNELS
    outer, rows = acc.shape[1], acc.shape[2]
    spans32[...] = spans_ref[...].astype(jnp.float32)

    def clear(a, carry):
        acc[:, a] = jnp.zeros((3, rows, LANES), jnp.float32)
        return carry

    lax.fori_loop(0, outer, clear, 0)
    band_iota = lax.broadcasted_iota(jnp.int32, (BAND, gal), 0).astype(jnp.float32)
    col_iota = lax.broadcasted_iota(jnp.int32, (SUBC, gal), 0).astype(jnp.float32)

    def one_span(j, carry):
        part = lambda n: spans32[pl.ds(j, 1), n * gal : (n + 1) * gal]
        hot = part(3) == band_iota
        weighted = jnp.concatenate(
            [jnp.where(hot, part(n), 0.0) for n in range(3)], axis=0
        ).astype(jnp.bfloat16)
        col_hot = jnp.where(part(4) == col_iota, 1.0, 0.0).astype(jnp.bfloat16)
        cells = lax.dot_general(
            weighted, col_hot, (((1,), (1,)), ((), ())), preferred_element_type=jnp.float32
        )
        a = block_ref[j]
        at = pl.ds(pl.multiple_of(band_ref[j] * BAND, BAND), BAND)
        for n in range(3):
            acc[n, a, at, :] += cells[n * BAND : (n + 1) * BAND]
        return carry

    lax.fori_loop(0, spans, one_span, 0, unroll=4)

    half = outer // 4
    side = side_ref[0]
    sign = (1 - 2 * side).astype(jnp.float32)

    def chunk(rc, carry):
        at = pl.ds(pl.multiple_of(rc * 8, 8), 8)
        points = ([], [])
        for a in range(half):
            x = []
            for c in range(4):
                inv = 1.0 / jnp.maximum(acc[0, a + c * half, at, :], 1.0)
                x.append((acc[1, a + c * half, at, :] * inv, acc[2, a + c * half, at, :] * inv))
            sum_r, sum_i = sign * (x[1][0] + x[3][0]), sign * (x[1][1] + x[3][1])
            dif_r, dif_i = sign * (x[1][0] - x[3][0]), sign * (x[1][1] - x[3][1])
            whole = (
                (x[0][0] + x[2][0] + sum_r, x[0][1] + x[2][1] + sum_i),
                (x[0][0] - x[2][0] + dif_i, x[0][1] - x[2][1] - dif_r),
            )
            for parity, (re, im) in enumerate(whole):
                base = ((side * 2 + parity) * half + a) * 2
                c, s = pre_ref[base], pre_ref[base + 1]
                points[parity].append((re * c - im * s, re * s + im * c))
        for parity in range(2):
            for m, (re, im) in enumerate(fft_list(points[parity], -1)):
                slot = parity * half + m
                c = tw_ref[side, slot : slot + 1, :]
                s = tw_ref[side, 2 * half + slot : 2 * half + slot + 1, :]
                mid[slot, at, :LANES] = re * c - im * s
                mid[slot, at, LANES:] = re * s + im * c
        return carry

    lax.fori_loop(0, rows // 8, chunk, 0)
    group = math.gcd(half, 4)
    for parity, out_ref in enumerate((even_ref, odd_ref)):

        def matmul(g, carry):
            hi, lo = split_hi_lo(
                mid[pl.ds(parity * half + g * group, group)].reshape(group * rows, 2 * LANES)
            )
            th, tl = table_ref[0], table_ref[1]
            res = dot(hi, th) + (dot(lo, th) + dot(hi, tl))
            out_ref[pl.ds(g * group, group)] = res.astype(jnp.bfloat16).reshape(
                group, rows, 2 * LANES
            )
            return carry

        lax.fori_loop(0, half // group, matmul, 0)


def cols_kernel(
    first_ref, in_ref, tw_ref, fwd_ref, inv_ref, out_ref, mid, *, total_cols, outer_cols
):
    _, rows, _ = in_ref.shape
    outer = 2 * mid.shape[0]
    inner = mid.shape[1] // 2
    per = inner // rows
    total_rows = outer * inner
    step = 16
    chunks = rows // step

    def place(t):
        h = t // chunks
        at = pl.ds(pl.multiple_of((t % chunks) * step, step), step)
        low = h * rows + (t % chunks) * step
        re_at = pl.ds(pl.multiple_of(low, step), step)
        im_at = pl.ds(pl.multiple_of(inner + low, step), step)
        return h, at, re_at, im_at

    def lanes(n):
        return slice(n % 2 * LANES, (n % 2 + 1) * LANES)

    def forward(t, carry):
        h, at, re_at, im_at = place(t)
        points = []
        for a in range(outer):
            both = in_ref[a * per + h, at, :].astype(jnp.float32)
            points.append((both[:, :LANES], both[:, LANES:]))
        for n, (re, im) in enumerate(fft_list(points, -1)):
            c = tw_ref[re_at, n : n + 1]
            s = tw_ref[re_at, outer + n : outer + n + 1]
            mid[n // 2, re_at, lanes(n)] = re * c - im * s
            mid[n // 2, im_at, lanes(n)] = re * s + im * c
        return carry

    lax.fori_loop(0, per * chunks, forward, 0)

    lane = lax.broadcasted_iota(jnp.int32, (1, 2 * LANES), 1)
    v = first_ref[0] + outer_cols * (lane % LANES)
    fx = jnp.where(v < total_cols // 2, v, v - total_cols).astype(jnp.float32) / total_cols

    def middle(n, carry):
        hi, lo = split_hi_lo(mid[n])
        th, tl = fwd_ref[0], fwd_ref[1]
        spec = dot(th, hi) + (dot(tl, hi) + dot(th, lo))
        sr, si = spec[:inner], spec[inner:]
        u = 2 * n + lane // LANES + outer * lax.broadcasted_iota(
            jnp.int32, (inner, 2 * LANES), 0
        )
        fy = jnp.where(u < total_rows // 2, u, u - total_rows).astype(jnp.float32) / total_rows
        fx2, fy2 = fx * fx, fy * fy
        radius = fx2 + fy2
        inv_radius = 1.0 / jnp.where(radius > 0, radius, 1.0)
        kr = (fx2 - fy2) * inv_radius
        ki = (2.0 * fx) * fy * inv_radius
        hat = jnp.concatenate([kr * sr + ki * si, kr * si - ki * sr], axis=0)
        hi, lo = split_hi_lo(hat)
        ih, il = inv_ref[0], inv_ref[1]
        mid[n] = dot(ih, hi) + (dot(il, hi) + dot(ih, lo))
        return carry

    lax.fori_loop(0, outer // 2, middle, 0)

    def backward(t, carry):
        h, at, re_at, im_at = place(t)
        points = []
        for n in range(outer):
            c = tw_ref[re_at, n : n + 1]
            s = tw_ref[re_at, outer + n : outer + n + 1]
            re = mid[n // 2, re_at, lanes(n)]
            im = mid[n // 2, im_at, lanes(n)]
            points.append((re * c + im * s, im * c - re * s))
        for a, (re, im) in enumerate(fft_list(points, 1)):
            out_ref[a * per + h, at, :LANES] = re.astype(jnp.bfloat16)
            out_ref[a * per + h, at, LANES:] = im.astype(jnp.bfloat16)
        return carry

    lax.fori_loop(0, per * chunks, backward, 0)


def back_matmul(in_ref, table_ref, mid):
    half, rows, _ = in_ref.shape
    group = math.gcd(half, 4)

    def matmul(g, carry):
        at = pl.ds(g * group, group)
        data = in_ref[at].reshape(group * rows, 2 * LANES)
        res = dot(data, table_ref[0]) + dot(data, table_ref[1])
        mid[at] = res.reshape(group, rows, 2 * LANES)
        return carry

    lax.fori_loop(0, half // group, matmul, 0)


def half_points(mid, tw_ref, at, parity):
    half = mid.shape[0]
    points = []
    for n in range(half):
        k = 2 * n + parity
        p = n % 2 * (half // 2) + n // 2
        c = tw_ref[k : k + 1, :]
        s = tw_ref[2 * half + k : 2 * half + k + 1, :]
        re = mid[p, at, :LANES]
        im = mid[p, at, LANES:]
        points.append((re * c + im * s, im * c - re * s))
    return fft_list(points, 1)


def back_even_kernel(in_ref, tw_ref, table_ref, out_ref, mid):
    back_matmul(in_ref, table_ref, mid)

    def chunk(rc, carry):
        at = pl.ds(pl.multiple_of(rc * 8, 8), 8)
        for a, (re, im) in enumerate(half_points(mid, tw_ref, at, 0)):
            out_ref[a, at, :LANES] = re
            out_ref[a, at, LANES:] = im
        return carry

    lax.fori_loop(0, in_ref.shape[1] // 8, chunk, 0)


def back_odd_kernel(in_ref, even_ref, tw_ref, table_ref, e_ref, b_ref, mid):
    back_matmul(in_ref, table_ref, mid)
    half = in_ref.shape[0]

    def chunk(rc, carry):
        at = pl.ds(pl.multiple_of(rc * 8, 8), 8)
        for a, (r, i) in enumerate(half_points(mid, tw_ref, at, 1)):
            c, s = math.cos(math.pi * a / half), math.sin(math.pi * a / half)
            tr, ti = r * c - i * s, r * s + i * c
            er, ei = even_ref[a, at, :LANES], even_ref[a, at, LANES:]
            low = slice(a * LANES, (a + 1) * LANES)
            high = slice((half + a) * LANES, (half + a + 1) * LANES)
            e_ref[at, low] = er + tr
            b_ref[at, low] = ei + ti
            e_ref[at, high] = er - tr
            b_ref[at, high] = ei - ti
        return carry

    lax.fori_loop(0, in_ref.shape[1] // 8, chunk, 0)


def vmem(count):
    return [pl.BlockSpec(memory_space=pltpu.VMEM)] * count


def smem():
    return pl.BlockSpec(memory_space=pltpu.SMEM)


def params():
    return pltpu.CompilerParams(vmem_limit_bytes=VMEM_BYTES)


def cost():
    return pl.CostEstimate(flops=4 * 10**9, bytes_accessed=8 * 2**20, transcendentals=0)


def exchange(x, groups=None):
    return lax.all_to_all(
        x, ("blk", "col"), split_axis=0, concat_axis=0, axis_index_groups=groups, tiled=True
    )


def fast_local(pixel_row, pixel_col, strip_of_span, shear_one, shear_two, weight):
    tile_count = lax.axis_size("col")
    devices = tile_count * lax.axis_size("blk")
    me = lax.axis_index("blk") * tile_count + lax.axis_index("col")
    spans, gal = pixel_row.shape
    depth = spans // devices
    rows = SLAB // tile_count
    total_rows = rows * devices
    total_cols = TILE_COLS * tile_count
    outer_x = total_cols // LANES
    outer_y = total_rows // LANES
    f32, bf16 = jnp.float32, jnp.bfloat16

    packed = pl.pallas_call(
        lambda *refs: pack_kernel(*refs, depth=depth),
        out_shape=jax.ShapeDtypeStruct((2 * spans, CHANNELS * gal), bf16),
        in_specs=vmem(6),
        out_specs=vmem(1)[0],
        compiler_params=params(),
        name="pack",
    )(pixel_row, pixel_col, strip_of_span, shear_one, shear_two, weight)
    mine = exchange(packed)
    group_size = devices // 2
    side, member = me // group_size, me % group_size
    groups = [[h * group_size + m for m in range(group_size)] for h in range(2)]
    tile_blocks = TILE_COLS // SUBC
    position = mine[:, 5 * gal].astype(jnp.int32)
    arrival = jnp.arange(2 * spans, dtype=jnp.int32)
    tile = arrival // (2 * depth) % tile_count
    block = tile * tile_blocks + position % tile_blocks
    band = arrival % (2 * depth) // depth * (rows // BAND) + position // tile_blocks

    tw_x = jnp.asarray(np.concatenate(np_twiddle(outer_x, LANES, -1), 0))
    c, s = np_twiddle(outer_y, LANES, -1)
    tw_y = np.zeros((LANES, max(LANES, 2 * outer_y)), np.float32)
    tw_y[:, :outer_y] = c.T
    tw_y[:, outer_y : 2 * outer_y] = s.T
    half = devices
    part = jax.ShapeDtypeStruct((group_size, 2 * rows, 2 * LANES), bf16)
    pre, side_tw = side_tables(outer_x)
    spectra = pl.pallas_call(
        rows_kernel,
        out_shape=[part, part],
        in_specs=[smem()] * 4 + vmem(3),
        out_specs=vmem(2),
        scratch_shapes=[
            pltpu.VMEM((2 * spans, CHANNELS * gal), f32),
            pltpu.VMEM((3, outer_x, 2 * rows, LANES), f32),
            pltpu.VMEM((outer_x // 2, 2 * rows, 2 * LANES), f32),
        ],
        compiler_params=params(),
        name="rows",
    )(
        block,
        band,
        jnp.full((1,), side, jnp.int32),
        jnp.asarray(pre),
        mine,
        jnp.asarray(side_tw),
        jnp.asarray(np_real_form(LANES, -1, 1.0, False)),
    )
    tw_y = jnp.asarray(tw_y)
    fwd_y = jnp.asarray(np_real_form(LANES, -1, 1.0, True))
    inv_y = jnp.asarray(np_real_form(LANES, 1, 1.0 / total_rows, True))
    inv_x = jnp.asarray(np_real_form(LANES, 1, 1.0 / total_cols, False))
    tag = ("even", "odd")
    cols = [exchange(spectra[j], groups) for j in range(2)]
    back = []
    for j in range(2):
        result = pl.pallas_call(
            lambda *refs: cols_kernel(*refs, total_cols=total_cols, outer_cols=outer_x),
            out_shape=part,
            in_specs=[smem()] + vmem(4),
            out_specs=vmem(1)[0],
            scratch_shapes=[pltpu.VMEM((outer_y // 2, 2 * LANES, 2 * LANES), f32)],
            compiler_params=params(),
            cost_estimate=cost(),
            name="cols_" + tag[j],
        )(jnp.full((1,), 4 * member + 2 * side + j, jnp.int32), cols[j], tw_y, fwd_y, inv_y)
        back.append(exchange(result.reshape(devices, rows, 2 * LANES)))
    scratch = [pltpu.VMEM((half, rows, 2 * LANES), f32)]
    even = pl.pallas_call(
        back_even_kernel,
        out_shape=jax.ShapeDtypeStruct((half, rows, 2 * LANES), f32),
        in_specs=vmem(3),
        out_specs=vmem(1)[0],
        scratch_shapes=scratch,
        compiler_params=params(),
        cost_estimate=cost(),
        name="back_even",
    )(back[0], tw_x, inv_x)
    return tuple(
        pl.pallas_call(
            back_odd_kernel,
            out_shape=[jax.ShapeDtypeStruct((rows, total_cols), f32)] * 2,
            in_specs=vmem(4),
            out_specs=vmem(2),
            scratch_shapes=scratch,
            compiler_params=params(),
            name="back_odd",
        )(back[1], even, tw_x, inv_x)
    )


def local(*args):
    tile_count = lax.axis_size("col")
    devices = tile_count * lax.axis_size("blk")
    if TILE_COLS * tile_count // LANES == 2 * devices:
        return fast_local(*args)
    return generic_local(*args)


def solution(mesh):
    placed = (
        P(("blk", "col"), None),
        P(("blk", "col"), None),
        P(("blk", "col"), None),
        P(("blk", "col"), None),
        P(("blk", "col"), None),
        P(("blk", "col"), None),
    )
    return jax.shard_map(
        local,
        mesh=mesh,
        in_specs=placed,
        out_specs=(P(("blk", "col"), None), P(("blk", "col"), None)),
        check_vma=False,
    )
```

profile of v0, /device:TPU:0, one launch (start us, length us, event | category | flops | bytes accessed | tf_op | source)
XLA Modules:
  0.0 148.8 jit_solution(9614157417805277120)
XLA Ops:
  0.6 2.1 %pack.1 = bf16[128,1536]{1,0:T(8,128)(2,1)} custom-call(s32[64,256]{1,0:T(8,128)} %refs_0_.1, s32[64,256]{1,0:T(8,128)} %refs_1_.1, s32[1,64]{1,0:T(1,128)} %refs_2_.3, f32[64,256]{1,0:T(8,128)} %refs_3_.3, f32[64,256]{1,0:T(8,128)} %refs_4_.3, f32[64,256]{1,0:T(8,128)} %refs_5_.1), custom_call_target="tpu_custom_call" | custom-call | tf_op jit(solution)/shard_map/pack/pallas_call | solution.py:572
  2.7 1.8 %all_to_all.19 = bf16[32,4,1536]{2,1,0:T(4,128)(2,1)} reshape(bf16[128,1536]{1,0:T(8,128)(2,1)} %pack.1) | data formatting | bytes 786432 | tf_op jit(solution)/shard_map/all_to_all | solution.py:554
  4.5 7.3 %all-to-all-start = ((bf16[32,4,1536]{2,1,0:T(4,128)(2,1)}), bf16[32,4,1536]{2,1,0:T(4,128)(2,1)S(1)}, u32[]{:S(2)}, u32[]{:S(2)}) async-start(bf16[32,4,1536]{2,1,0:T(4,128)(2,1)} %all_to_all.19), calls=%async_computation | async-start | bytes 786432 | tf_op jit(solution)/shard_map/all_to_all | solution.py:554
  11.9 13.2 %all-to-all-done = bf16[32,4,1536]{2,1,0:T(4,128)(2,1)S(1)} async-done(((bf16[32,4,1536]{2,1,0:T(4,128)(2,1)}), bf16[32,4,1536]{2,1,0:T(4,128)(2,1)S(1)}, u32[]{:S(2)}, u32[]{:S(2)}) %all-to-all-start) | async-done | bytes 393248 | tf_op jit(solution)/shard_map/all_to_all | solution.py:554
  25.1 0.1 all_to_all.21.spans_ref
  25.2 0.0 copy-start.1
  25.2 0.1 convert_reduce_fusion
  25.3 0.6 multiply_add_fusion
  25.9 0.0 copy-done.1
  25.9 16.0 %rows.1 = (bf16[16,128,256]{2,1,0:T(8,128)(2,1)}, bf16[16,128,256]{2,1,0:T(8,128)(2,1)}) custom-call(s32[128]{0:T(128)} %get-tuple-element.7.block_ref, s32[128]{0:T(128)} %get-tuple-element.6.band_ref, s32[1]{0:T(128)} %bitcast.1.side_ref, f32[128]{0:T(128)} %constant.109.clone.pre_ref, bf16[128,1536]{1,0:T(8,128)(2,1)} %copy-done.1, ...), custom_call_target="tpu_custom_call" | custom-call | tf_op jit(solution)/shard_map/rows/pallas_call | solution.py:599
  42.0 20.5 %all_to_all.31.refs_1_ = bf16[16,128,256]{2,1,0:T(8,128)(2,1)} all-to-all(bf16[16,128,256]{2,1,0:T(8,128)(2,1)} %get-tuple-element.5), channel_id=1, replica_groups={{0,1,2,3,4,5,6,7,8,9,10,11,12,13,14,15},{16,17,18,19,20,21,22,23,24,25,..., dimensions={0} | all-to-all | bytes 2097152 | tf_op jit(solution)/shard_map/all_to_all | solution.py:554
  62.4 3.7 %all-to-all-start.1 = ((bf16[16,128,256]{2,1,0:T(8,128)(2,1)}), bf16[16,128,256]{2,1,0:T(8,128)(2,1)S(1)}, u32[]{:S(2)}, u32[]{:S(2)}) async-start(bf16[16,128,256]{2,1,0:T(8,128)(2,1)} %get-tuple-element.4), calls=%async_computation.1 | async-start | bytes 2097152 | tf_op jit(solution)/shard_map/all_to_all | solution.py:554
  66.1 11.2 %cols_even.1 = bf16[16,128,256]{2,1,0:T(8,128)(2,1)} custom-call(s32[1]{0:T(128)} %bitcast.3.refs_0_, bf16[16,128,256]{2,1,0:T(8,128)(2,1)} %all_to_all.31.refs_1_, f32[128,128]{1,0:T(8,128)} %constant.112.clone.refs_2_, bf16[2,256,256]{2,1,0:T(8,128)(2,1)} %constant.113.clone.refs_3_, bf16[2,256,256]{2,1,0:T(8,128)(2,1)} %constant.114.clone.refs_4_), custom_call_target="tpu_custom_call" | custom-call | flops 4000000000 | bytes 8388608 | tf_op jit(solution)/shard_map/cols_even/pallas_call | solution.py:628
  77.3 4.9 %all-to-all-done.1.refs_1_ = bf16[16,128,256]{2,1,0:T(8,128)(2,1)S(1)} async-done(((bf16[16,128,256]{2,1,0:T(8,128)(2,1)}), bf16[16,128,256]{2,1,0:T(8,128)(2,1)S(1)}, u32[]{:S(2)}, u32[]{:S(2)}) %all-to-all-start.1) | async-done | bytes 1048608 | tf_op jit(solution)/shard_map/all_to_all | solution.py:554
  82.2 2.6 %all-to-all-start.4 = ((bf16[32,64,256]{2,1,0:T(8,128)(2,1)}), bf16[32,64,256]{2,1,0:T(8,128)(2,1)S(1)}, u32[]{:S(2)}, u32[]{:S(2)}) async-start(bf16[32,64,256]{2,1,0:T(8,128)(2,1)} %bitcast.5), calls=%async_computation.4 | async-start | bytes 2097152 | tf_op jit(solution)/shard_map/all_to_all | solution.py:554
  84.9 0.0 copy-done.2
  84.9 11.2 %cols_odd.1 = bf16[16,128,256]{2,1,0:T(8,128)(2,1)} custom-call(s32[1]{0:T(128)} %bitcast.refs_0_, bf16[16,128,256]{2,1,0:T(8,128)(2,1)} %copy-done.2, f32[128,128]{1,0:T(8,128)} %constant.112.clone.refs_2_, bf16[2,256,256]{2,1,0:T(8,128)(2,1)} %constant.113.clone.refs_3_, bf16[2,256,256]{2,1,0:T(8,128)(2,1)} %constant.114.clone.refs_4_), custom_call_target="tpu_custom_call" | custom-call | flops 4000000000 | bytes 8388608 | tf_op jit(solution)/shard_map/cols_odd/pallas_call | solution.py:628
  96.1 15.0 %all-to-all-done.4.in_ref = bf16[32,64,256]{2,1,0:T(8,128)(2,1)S(1)} async-done(((bf16[32,64,256]{2,1,0:T(8,128)(2,1)}), bf16[32,64,256]{2,1,0:T(8,128)(2,1)S(1)}, u32[]{:S(2)}, u32[]{:S(2)}) %all-to-all-start.4) | async-done | bytes 1048608 | tf_op jit(solution)/shard_map/all_to_all | solution.py:554
  111.1 3.5 %all-to-all-start.2 = ((bf16[32,64,256]{2,1,0:T(8,128)(2,1)}), bf16[32,64,256]{2,1,0:T(8,128)(2,1)S(1)}, u32[]{:S(2)}, u32[]{:S(2)}) async-start(bf16[32,64,256]{2,1,0:T(8,128)(2,1)} %bitcast.6), calls=%async_computation.2 | async-start | bytes 2097152 | tf_op jit(solution)/shard_map/all_to_all | solution.py:554
  114.6 0.0 copy-done.3
  114.6 5.4 %back_even.1.even_ref = f32[32,64,256]{2,1,0:T(8,128)} custom-call(bf16[32,64,256]{2,1,0:T(8,128)(2,1)} %copy-done.3, f32[128,128]{1,0:T(8,128)} %constant.108.clone.tw_ref, bf16[2,256,256]{2,1,0:T(8,128)(2,1)} %constant.115.clone.table_ref), custom_call_target="tpu_custom_call" | custom-call | flops 4000000000 | bytes 8388608 | tf_op jit(solution)/shard_map/back_even/pallas_call | solution.py:640
  120.0 20.8 %all-to-all-done.2.in_ref = bf16[32,64,256]{2,1,0:T(8,128)(2,1)S(1)} async-done(((bf16[32,64,256]{2,1,0:T(8,128)(2,1)}), bf16[32,64,256]{2,1,0:T(8,128)(2,1)S(1)}, u32[]{:S(2)}, u32[]{:S(2)}) %all-to-all-start.2) | async-done | bytes 1048608 | tf_op jit(solution)/shard_map/all_to_all | solution.py:554
  140.8 1.0 copy-done
  141.8 7.0 %back_odd.1 = (f32[64,8192]{1,0:T(8,128)}, f32[64,8192]{1,0:T(8,128)}) custom-call(bf16[32,64,256]{2,1,0:T(8,128)(2,1)} %copy-done, f32[32,64,256]{2,1,0:T(8,128)} %back_even.1.even_ref, f32[128,128]{1,0:T(8,128)} %constant.108.clone.tw_ref, bf16[2,256,256]{2,1,0:T(8,128)(2,1)} %constant.115.clone.table_ref), custom_call_target="tpu_custom_call" | custom-call | tf_op jit(solution)/shard_map/back_odd/pallas_call | solution.py:651
  (3 shorter events, 0.0 us)
Async XLA Ops:
  4.5 20.6 %all-to-all-start = ((bf16[32,4,1536]{2,1,0:T(4,128)(2,1)}), bf16[32,4,1536]{2,1,0:T(4,128)(2,1)S(1)}, u32[]{:S(2)}, u32[]{:S(2)}) async-start(bf16[32,4,1536]{2,1,0:T(4,128)(2,1)} %all_to_all.19), calls=%async_computation | async-start | bytes 786432 | tf_op jit(solution)/shard_map/all_to_all | solution.py:554
  25.2 0.7 copy-start.1
  62.4 19.8 %all-to-all-start.1 = ((bf16[16,128,256]{2,1,0:T(8,128)(2,1)}), bf16[16,128,256]{2,1,0:T(8,128)(2,1)S(1)}, u32[]{:S(2)}, u32[]{:S(2)}) async-start(bf16[16,128,256]{2,1,0:T(8,128)(2,1)} %get-tuple-element.4), calls=%async_computation.1 | async-start | bytes 2097152 | tf_op jit(solution)/shard_map/all_to_all | solution.py:554
  82.2 2.7 %copy-start.2 = (bf16[16,128,256]{2,1,0:T(8,128)(2,1)}, bf16[16,128,256]{2,1,0:T(8,128)(2,1)S(1)}, u32[]{:S(2)}) copy-start(bf16[16,128,256]{2,1,0:T(8,128)(2,1)S(1)} %all-to-all-done.1.refs_1_) | copy-start | bytes 3145732
  82.2 28.8 %all-to-all-start.4 = ((bf16[32,64,256]{2,1,0:T(8,128)(2,1)}), bf16[32,64,256]{2,1,0:T(8,128)(2,1)S(1)}, u32[]{:S(2)}, u32[]{:S(2)}) async-start(bf16[32,64,256]{2,1,0:T(8,128)(2,1)} %bitcast.5), calls=%async_computation.4 | async-start | bytes 2097152 | tf_op jit(solution)/shard_map/all_to_all | solution.py:554
  111.1 3.6 %copy-start.3 = (bf16[32,64,256]{2,1,0:T(8,128)(2,1)}, bf16[32,64,256]{2,1,0:T(8,128)(2,1)S(1)}, u32[]{:S(2)}) copy-start(bf16[32,64,256]{2,1,0:T(8,128)(2,1)S(1)} %all-to-all-done.4.in_ref) | copy-start | bytes 3145732
  111.1 29.8 %all-to-all-start.2 = ((bf16[32,64,256]{2,1,0:T(8,128)(2,1)}), bf16[32,64,256]{2,1,0:T(8,128)(2,1)S(1)}, u32[]{:S(2)}, u32[]{:S(2)}) async-start(bf16[32,64,256]{2,1,0:T(8,128)(2,1)} %bitcast.6), calls=%async_computation.2 | async-start | bytes 2097152 | tf_op jit(solution)/shard_map/all_to_all | solution.py:554
  140.8 1.0 copy-start
where the time goes:
time: 150 us; the launch traced here: 149 us
  waiting for transfers between devices  54 us (36%)
  Pallas kernels  52.8 us (35%)
  blocking collectives  20.5 us (14%)
  starting transfers between devices  17.2 us (11%)
  local copies, waits for them, and re-layouts  2.94 us (2%)
    all_to_all x4, waiting for transfers between devices, exchange(): lax.all_to_all(x, ('blk', 'col'), split_axis=0, concat_axis=0, axis_index...  54 us
    pallas_call x2, Pallas kernels, fast_local(): pl.pallas_call(lambda *refs: cols_kernel(*refs, total_cols=total_cols, ou...  22.4 us
    all_to_all x1, blocking collectives, exchange(): lax.all_to_all(x, ('blk', 'col'), split_axis=0, concat_axis=0, axis_index...  20.5 us
    all_to_all x4, starting transfers between devices, exchange(): lax.all_to_all(x, ('blk', 'col'), split_axis=0, concat_axis=0, axis_index...  17.2 us
    pallas_call x1, Pallas kernels, fast_local(): pl.pallas_call(rows_kernel, out_shape=[part, part], in_specs=[smem()] * 4...  16 us
    pallas_call x1, Pallas kernels, fast_local(): pl.pallas_call(back_odd_kernel, out_shape=[jax.ShapeDtypeStruct((rows, to...  6.98 us
    pallas_call x1, Pallas kernels, fast_local(): pl.pallas_call(back_even_kernel, out_shape=jax.ShapeDtypeStruct((half, ro...  5.37 us
  transfers between devices with their start and end apart: 4, of which 4 were waited for; matrix products, arithmetic and copies ran while one was open for 0% of the time, Pallas kernels for 19%

commit v1 on v0

--- a/solution.py
+++ b/solution.py
@@ -16,6 +16,7 @@
 
 
 highest = lax.Precision.HIGHEST
+MESH = pl.DeviceIdType.MESH
 
 
 def factor_pair(length):
@@ -392,23 +393,23 @@
         lax.fori_loop(0, half // group, matmul, 0)
 
 
-def cols_kernel(
-    first_ref, in_ref, tw_ref, fwd_ref, inv_ref, out_ref, mid, *, total_cols, outer_cols
-):
-    _, rows, _ = in_ref.shape
+def cols_transform(in_ref, tw_ref, fwd_ref, inv_ref, out_ref, mid, first, total_cols, outer_cols):
+    rows = in_ref.shape[1]
+    out_rows = out_ref.shape[1]
     outer = 2 * mid.shape[0]
     inner = mid.shape[1] // 2
     per = inner // rows
+    out_per = inner // out_rows
     total_rows = outer * inner
     step = 16
     chunks = rows // step
+    out_chunks = out_rows // step
 
     def place(t):
         h = t // chunks
         at = pl.ds(pl.multiple_of((t % chunks) * step, step), step)
-        low = h * rows + (t % chunks) * step
-        re_at = pl.ds(pl.multiple_of(low, step), step)
-        im_at = pl.ds(pl.multiple_of(inner + low, step), step)
+        re_at = pl.ds(pl.multiple_of(t * step, step), step)
+        im_at = pl.ds(pl.multiple_of(inner + t * step, step), step)
         return h, at, re_at, im_at
 
     def lanes(n):
@@ -427,10 +428,10 @@
             mid[n // 2, im_at, lanes(n)] = re * s + im * c
         return carry
 
-    lax.fori_loop(0, per * chunks, forward, 0)
+    lax.fori_loop(0, inner // step, forward, 0)
 
     lane = lax.broadcasted_iota(jnp.int32, (1, 2 * LANES), 1)
-    v = first_ref[0] + outer_cols * (lane % LANES)
+    v = first + outer_cols * (lane % LANES)
     fx = jnp.where(v < total_cols // 2, v, v - total_cols).astype(jnp.float32) / total_cols
 
     def middle(n, carry):
@@ -456,7 +457,9 @@
     lax.fori_loop(0, outer // 2, middle, 0)
 
     def backward(t, carry):
-        h, at, re_at, im_at = place(t)
+        _, _, re_at, im_at = place(t)
+        h = t // out_chunks
+        at = pl.ds(pl.multiple_of((t % out_chunks) * step, step), step)
         points = []
         for n in range(outer):
             c = tw_ref[re_at, n : n + 1]
@@ -465,11 +468,85 @@
             im = mid[n // 2, im_at, lanes(n)]
             points.append((re * c + im * s, im * c - re * s))
         for a, (re, im) in enumerate(fft_list(points, 1)):
-            out_ref[a * per + h, at, :LANES] = re.astype(jnp.bfloat16)
-            out_ref[a * per + h, at, LANES:] = im.astype(jnp.bfloat16)
-        return carry
-
-    lax.fori_loop(0, per * chunks, backward, 0)
+            out_ref[a * out_per + h, at, :LANES] = re.astype(jnp.bfloat16)
+            out_ref[a * out_per + h, at, LANES:] = im.astype(jnp.bfloat16)
+        return carry
+
+    lax.fori_loop(0, inner // step, backward, 0)
+
+
+def spectral_kernel(
+    even_ref, odd_ref, tw_ref, fwd_ref, inv_ref, back_even_ref, back_odd_ref,
+    cols, results, mid, fwd_send, fwd_recv, back_send, back_recv, *, total_cols, outer_cols
+):
+    tile_count = lax.axis_size("col")
+    devices = tile_count * lax.axis_size("blk")
+    me = lax.axis_index("blk") * tile_count + lax.axis_index("col")
+    group = devices // 2
+    side, member = me // group, me % group
+    sources = (even_ref, odd_ref)
+    backs = (back_even_ref, back_odd_ref)
+
+    def place(device):
+        return (device // tile_count, device % tile_count)
+
+    barrier = pltpu.get_barrier_semaphore()
+
+    def greet(k, carry):
+        pl.semaphore_signal(
+            barrier, inc=1, device_id=place((me + k) % devices), device_id_type=MESH
+        )
+        return carry
+
+    lax.fori_loop(1, devices, greet, 0)
+    pl.semaphore_wait(barrier, devices - 1)
+
+    def forward(j, k):
+        to = (member + k) % group
+        return pltpu.make_async_remote_copy(
+            src_ref=sources[j].at[to],
+            dst_ref=cols.at[j, member],
+            send_sem=fwd_send.at[j, k],
+            recv_sem=fwd_recv.at[j, k],
+            device_id=place(side * group + to),
+            device_id_type=MESH,
+        )
+
+    def backward(j, k):
+        to = (me + k) % devices
+        return pltpu.make_async_remote_copy(
+            src_ref=results.at[j, to],
+            dst_ref=backs[j].at[me],
+            send_sem=back_send.at[j, k],
+            recv_sem=back_recv.at[j, k],
+            device_id=place(to),
+            device_id_type=MESH,
+        )
+
+    def every(copy, j, count, act):
+        def one(k, carry):
+            act(copy(j, k))
+            return carry
+
+        lax.fori_loop(1, count, one, 0)
+
+    for j in range(2):
+        every(forward, j, group, lambda c: c.start())
+    for j in range(2):
+        cols[j, member] = sources[j][member]
+    for j in range(2):
+        every(forward, j, group, lambda c: c.wait_recv())
+        cols_transform(
+            cols.at[j], tw_ref, fwd_ref, inv_ref, results.at[j], mid,
+            4 * member + 2 * side + j, total_cols, outer_cols,
+        )
+        every(backward, j, devices, lambda c: c.start())
+        backs[j][me] = results[j, me]
+    for j in range(2):
+        every(backward, j, devices, lambda c: c.wait_recv())
+    for j in range(2):
+        every(forward, j, group, lambda c: c.wait_send())
+        every(backward, j, devices, lambda c: c.wait_send())
 
 
 def back_matmul(in_ref, table_ref, mid):
@@ -621,21 +698,26 @@
     fwd_y = jnp.asarray(np_real_form(LANES, -1, 1.0, True))
     inv_y = jnp.asarray(np_real_form(LANES, 1, 1.0 / total_rows, True))
     inv_x = jnp.asarray(np_real_form(LANES, 1, 1.0 / total_cols, False))
-    tag = ("even", "odd")
-    cols = [exchange(spectra[j], groups) for j in range(2)]
-    back = []
-    for j in range(2):
-        result = pl.pallas_call(
-            lambda *refs: cols_kernel(*refs, total_cols=total_cols, outer_cols=outer_x),
-            out_shape=part,
-            in_specs=[smem()] + vmem(4),
-            out_specs=vmem(1)[0],
-            scratch_shapes=[pltpu.VMEM((outer_y // 2, 2 * LANES, 2 * LANES), f32)],
-            compiler_params=params(),
-            cost_estimate=cost(),
-            name="cols_" + tag[j],
-        )(jnp.full((1,), 4 * member + 2 * side + j, jnp.int32), cols[j], tw_y, fwd_y, inv_y)
-        back.append(exchange(result.reshape(devices, rows, 2 * LANES)))
+    dma = pltpu.SemaphoreType.DMA
+    back = pl.pallas_call(
+        lambda *refs: spectral_kernel(*refs, total_cols=total_cols, outer_cols=outer_x),
+        out_shape=[jax.ShapeDtypeStruct((devices, rows, 2 * LANES), bf16)] * 2,
+        in_specs=vmem(5),
+        out_specs=vmem(2),
+        scratch_shapes=[
+            pltpu.VMEM((2, group_size, 2 * rows, 2 * LANES), bf16),
+            pltpu.VMEM((2, devices, rows, 2 * LANES), bf16),
+            pltpu.VMEM((outer_y // 2, 2 * LANES, 2 * LANES), f32),
+            dma((2, group_size)),
+            dma((2, group_size)),
+            dma((2, devices)),
+            dma((2, devices)),
+        ],
+        compiler_params=pltpu.CompilerParams(
+            vmem_limit_bytes=VMEM_BYTES, collective_id=1, has_side_effects=True
+        ),
+        name="spectral",
+    )(spectra[0], spectra[1], tw_y, fwd_y, inv_y)
     scratch = [pltpu.VMEM((half, rows, 2 * LANES), f32)]
     even = pl.pallas_call(
         back_even_kernel,

time: 150 us -> 133 us (0.89)
  the two profiles are of different devices: /device:TPU:0 before, /device:TPU:11 now
where the time goes in v1:
time: 133 us; the launch traced here: 132 us
  Pallas kernels  111 us (83%)
  waiting for transfers between devices  11.3 us (8%)
  starting transfers between devices  6.3 us (5%)
  local copies, waits for them, and re-layouts  1.94 us (1%)
    pallas_call x1, Pallas kernels, fast_local(): pl.pallas_call(lambda *refs: spectral_kernel(*refs, total_cols=total_cols...  81 us
    pallas_call x1, Pallas kernels, fast_local(): pl.pallas_call(rows_kernel, out_shape=[part, part], in_specs=[smem()] * 4...  16 us
    all_to_all x1, waiting for transfers between devices, exchange(): lax.all_to_all(x, ('blk', 'col'), split_axis=0, concat_axis=0, axis_index...  11.3 us
    pallas_call x1, Pallas kernels, fast_local(): pl.pallas_call(back_odd_kernel, out_shape=[jax.ShapeDtypeStruct((rows, to...  6.98 us
    all_to_all x1, starting transfers between devices, exchange(): lax.all_to_all(x, ('blk', 'col'), split_axis=0, concat_axis=0, axis_index...  6.3 us
    pallas_call x1, Pallas kernels, fast_local(): pl.pallas_call(back_even_kernel, out_shape=jax.ShapeDtypeStruct((half, ro...  5.37 us
  transfers between devices with their start and end apart: 1, of which 1 were waited for; matrix products, arithmetic and copies ran while one was open for 0% of the time, Pallas kernels for 0%

profile of v1, /device:TPU:11, one launch (start us, length us, event | category | flops | bytes accessed | tf_op | source)
XLA Modules:
  0.0 132.4 jit_solution(11000735151099567194)
XLA Ops:
  0.6 2.1 %pack.1 = bf16[128,1536]{1,0:T(8,128)(2,1)} custom-call(s32[64,256]{1,0:T(8,128)} %refs_0_.1, s32[64,256]{1,0:T(8,128)} %refs_1_.1, s32[1,64]{1,0:T(1,128)} %refs_2_.2, f32[64,256]{1,0:T(8,128)} %refs_3_.2, f32[64,256]{1,0:T(8,128)} %refs_4_.2, f32[64,256]{1,0:T(8,128)} %refs_5_.1), custom_call_target="tpu_custom_call" | custom-call | tf_op jit(solution)/shard_map/pack/pallas_call | solution.py:649
  2.7 1.8 %all_to_all.7 = bf16[32,4,1536]{2,1,0:T(4,128)(2,1)} reshape(bf16[128,1536]{1,0:T(8,128)(2,1)} %pack.1) | data formatting | bytes 786432 | tf_op jit(solution)/shard_map/all_to_all | solution.py:631
  4.5 6.3 %all-to-all-start = ((bf16[32,4,1536]{2,1,0:T(4,128)(2,1)}), bf16[32,4,1536]{2,1,0:T(4,128)(2,1)S(1)}, u32[]{:S(2)}, u32[]{:S(2)}) async-start(bf16[32,4,1536]{2,1,0:T(4,128)(2,1)} %all_to_all.7), calls=%async_computation | async-start | bytes 786432 | tf_op jit(solution)/shard_map/all_to_all | solution.py:631
  10.8 11.3 %all-to-all-done = bf16[32,4,1536]{2,1,0:T(4,128)(2,1)S(1)} async-done(((bf16[32,4,1536]{2,1,0:T(4,128)(2,1)}), bf16[32,4,1536]{2,1,0:T(4,128)(2,1)S(1)}, u32[]{:S(2)}, u32[]{:S(2)}) %all-to-all-start) | async-done | bytes 393248 | tf_op jit(solution)/shard_map/all_to_all | solution.py:631
  22.2 0.1 all_to_all.9.spans_ref
  22.3 0.0 copy-start
  22.3 0.1 convert_reduce_fusion
  22.4 0.6 multiply_add_fusion
  23.0 0.0 copy-done
  23.0 16.0 %rows.1 = (bf16[16,128,256]{2,1,0:T(8,128)(2,1)}, bf16[16,128,256]{2,1,0:T(8,128)(2,1)}) custom-call(s32[128]{0:T(128)} %get-tuple-element.11.block_ref, s32[128]{0:T(128)} %get-tuple-element.10.band_ref, s32[1]{0:T(128)} %bitcast.side_ref, f32[128]{0:T(128)} %constant.102.clone.pre_ref, bf16[128,1536]{1,0:T(8,128)(2,1)} %copy-done, ...), custom_call_target="tpu_custom_call" | custom-call | tf_op jit(solution)/shard_map/rows/pallas_call | solution.py:676
  39.1 81.0 %spectral.1 = (bf16[32,64,256]{2,1,0:T(8,128)(2,1)}, bf16[32,64,256]{2,1,0:T(8,128)(2,1)}) custom-call(bf16[16,128,256]{2,1,0:T(8,128)(2,1)} %get-tuple-element.6.refs_0_, bf16[16,128,256]{2,1,0:T(8,128)(2,1)} %get-tuple-element.7.refs_1_, f32[128,128]{1,0:T(8,128)} %constant.105.clone.refs_2_, bf16[2,256,256]{2,1,0:T(8,128)(2,1)} %constant.106.clone.refs_3_, ...), custom_call_target="tpu_custom_call" | custom-call | tf_op jit(solution)/shard_map/spectral/pallas_call | solution.py:702
  120.0 5.4 %back_even.1.even_ref = f32[32,64,256]{2,1,0:T(8,128)} custom-call(bf16[32,64,256]{2,1,0:T(8,128)(2,1)} %get-tuple-element.9.in_ref, f32[128,128]{1,0:T(8,128)} %constant.101.clone.tw_ref, bf16[2,256,256]{2,1,0:T(8,128)(2,1)} %constant.108.clone.table_ref), custom_call_target="tpu_custom_call" | custom-call | flops 4000000000 | bytes 8388608 | tf_op jit(solution)/shard_map/back_even/pallas_call | solution.py:722
  125.4 7.0 %back_odd.1 = (f32[64,8192]{1,0:T(8,128)}, f32[64,8192]{1,0:T(8,128)}) custom-call(bf16[32,64,256]{2,1,0:T(8,128)(2,1)} %get-tuple-element.8.in_ref, f32[32,64,256]{2,1,0:T(8,128)} %back_even.1.even_ref, f32[128,128]{1,0:T(8,128)} %constant.101.clone.tw_ref, bf16[2,256,256]{2,1,0:T(8,128)(2,1)} %constant.108.clone.table_ref), custom_call_target="tpu_custom_call" | custom-call | tf_op jit(solution)/shard_map/back_odd/pallas_call | solution.py:733
Async XLA Ops:
  4.5 17.7 %all-to-all-start = ((bf16[32,4,1536]{2,1,0:T(4,128)(2,1)}), bf16[32,4,1536]{2,1,0:T(4,128)(2,1)S(1)}, u32[]{:S(2)}, u32[]{:S(2)}) async-start(bf16[32,4,1536]{2,1,0:T(4,128)(2,1)} %all_to_all.7), calls=%async_computation | async-start | bytes 786432 | tf_op jit(solution)/shard_map/all_to_all | solution.py:631
  22.3 0.8 copy-start
